TPU v7x, 8 devices: a whole 2x2x1 slice. The times are simulated.
8 devices in a mesh: rep: 1 (over z), data: 2 (over y), expert: 4 (over x, core).
Axes of the slice: x: 2, y: 2, z: 1, core: 2. Of those that a mesh axis runs over, the one named last changes fastest.
Arguments:
- x: bfloat16 [128, 128, 2304], P(('rep', 'expert', 'data'))
- expert_idx: int32 [128, 128, 2], P(('rep', 'expert', 'data'))
- gate: float32 [128, 128, 2], P(('rep', 'expert', 'data'))
- attn_gain: float32 [2304], replicated
- w_qkv: bfloat16 [2304, 108, 64], P(('data', 'expert'))
- w_out: bfloat16 [36, 64, 2304], P(None, None, ('data', 'expert'))
- moe_gain: float32 [2304], replicated
- w_gate: bfloat16 [8, 2304, 5760], P('expert', 'data')
- w_up: bfloat16 [8, 2304, 5760], P('expert', 'data')
- w_down: bfloat16 [8, 5760, 2304], P('expert', None, 'data')
Outputs:
- output: bfloat16 [128, 128, 2304], P(('rep', 'expert', 'data'))
All inputs are finite; a program needn't handle non-finite values.
Results may differ from a plain program's by a relative error of at most 0.0147271.
Values are sent between devices in bfloat16 or wider.
A program may use at most 1 GiB of HBM per device.

v0:
```python
import jax
import jax.numpy as jnp
from jax import lax
from jax.sharding import PartitionSpec as P

NORM_EPS = 1e-6
ROPE_BASE = 10000.0


def rms_scale(tok_rows, gain):
    rows_f32 = tok_rows.astype(jnp.float32)
    inv_rms = lax.rsqrt(jnp.mean(rows_f32 * rows_f32, axis=-1, keepdims=True) + NORM_EPS)
    return (rows_f32 * inv_rms * gain).astype(jnp.bfloat16)


def rope_apply(head_vals):
    seq_len, head_dim = head_vals.shape[1], head_vals.shape[-1]
    half_dim = head_dim // 2
    inv_freq = ROPE_BASE ** (-jnp.arange(half_dim, dtype=jnp.float32) * 2.0 / head_dim)
    angles = jnp.arange(seq_len, dtype=jnp.float32)[:, None] * inv_freq[None, :]
    cos_b = jnp.cos(angles)[None, :, None, :]
    sin_b = jnp.sin(angles)[None, :, None, :]
    vals_f32 = head_vals.astype(jnp.float32)
    low_half = vals_f32[..., :half_dim]
    high_half = vals_f32[..., half_dim:]
    return jnp.concatenate([low_half * cos_b - high_half * sin_b, high_half * cos_b + low_half * sin_b], axis=-1).astype(jnp.bfloat16)


def attention_block(seqs, attn_gain, w_qkv, w_out):
    num_seqs, seq_len, model_dim = seqs.shape
    head_dim = w_qkv.shape[2]
    num_heads = w_out.shape[0]
    kv_heads = (w_qkv.shape[1] - num_heads) // 2
    group_len = num_heads // kv_heads
    normed = rms_scale(seqs, attn_gain)
    qkv_all = jnp.einsum('uno,ojf->unjf', normed, w_qkv, preferred_element_type=jnp.float32).astype(jnp.bfloat16)
    queries = rope_apply(qkv_all[:, :, :num_heads]).reshape(num_seqs, seq_len, kv_heads, group_len, head_dim)
    keys_rot = rope_apply(qkv_all[:, :, num_heads:num_heads + kv_heads])
    values = qkv_all[:, :, num_heads + kv_heads:]
    scores = jnp.einsum('slkgd,smkd->skglm', queries, keys_rot, preferred_element_type=jnp.float32) * (head_dim ** -0.5)
    causal = lax.broadcasted_iota(jnp.int32, (seq_len, seq_len), 0) >= lax.broadcasted_iota(jnp.int32, (seq_len, seq_len), 1)
    attn_probs = jax.nn.softmax(jnp.where(causal, scores, -1e30), axis=-1).astype(jnp.bfloat16)
    mixed = jnp.einsum('skglm,smkd->slkgd', attn_probs, values, preferred_element_type=jnp.float32).astype(jnp.bfloat16)
    out_grouped = w_out.reshape(kv_heads, group_len, head_dim, model_dim)
    attn_proj = jnp.einsum('slkgd,kgdm->slm', mixed, out_grouped, preferred_element_type=jnp.float32)
    return (seqs.astype(jnp.float32) + attn_proj).astype(jnp.bfloat16)


def capacity_of(tok_dev, top_k, num_experts):
    return 8 * ((5 * top_k * tok_dev + 32 * num_experts - 1) // (32 * num_experts))


def dispatch_target(flat_ids, num_experts, capacity):
    onehot = (flat_ids[:, None] == jnp.arange(num_experts, dtype=jnp.int32)[None, :]).astype(jnp.int32)
    earlier = jnp.cumsum(onehot, axis=0) - onehot
    slot_pos = jnp.sum(earlier * onehot, axis=1)
    return jnp.where(slot_pos < capacity, flat_ids * capacity + slot_pos, num_experts * capacity)


def gather_rows(normed, target_rows, num_experts, capacity, top_k):
    tok_dev = normed.shape[0]
    source = jnp.full((num_experts * capacity + 1,), tok_dev, jnp.int32)
    source = source.at[target_rows].set(jnp.arange(tok_dev * top_k, dtype=jnp.int32) // top_k)
    padded = jnp.concatenate([normed, jnp.zeros((1, normed.shape[1]), normed.dtype)], axis=0)
    return jnp.take(padded, source[:num_experts * capacity], axis=0)


def combine_rows(expert_rows, target_rows, gate_rows):
    tok_dev, top_k = gate_rows.shape
    padded = jnp.concatenate([expert_rows, jnp.zeros((1, expert_rows.shape[1]), expert_rows.dtype)], axis=0)
    picked = jnp.take(padded, target_rows, axis=0).reshape(tok_dev, top_k, expert_rows.shape[1])
    return jnp.sum(picked.astype(jnp.float32) * gate_rows[:, :, None], axis=1)


def solution(mesh):
    expert_size = mesh.shape['expert']
    tok_spec = P(('rep', 'expert', 'data'), None, None)
    group_axes = ('data', 'expert')

    def local_step(x_loc, idx_loc, gate_loc, attn_gain, qkv_part, out_part, moe_gain, gate_part, up_part, down_part):
        w_qkv = lax.all_gather(qkv_part, group_axes, axis=0, tiled=True)
        w_out = lax.all_gather(out_part, group_axes, axis=2, tiled=True)
        hidden = attention_block(x_loc, attn_gain, w_qkv, w_out)
        num_seqs, seq_len, model_dim = hidden.shape
        tok_dev = num_seqs * seq_len
        top_k = idx_loc.shape[-1]
        loc_experts = gate_part.shape[0]
        num_experts = loc_experts * expert_size
        capacity = capacity_of(tok_dev, top_k, num_experts)
        flat_hidden = hidden.reshape(tok_dev, model_dim)
        normed = rms_scale(flat_hidden, moe_gain)
        target_rows = dispatch_target(idx_loc.reshape(tok_dev * top_k), num_experts, capacity)
        send_buf = gather_rows(normed, target_rows, num_experts, capacity, top_k).reshape(expert_size, loc_experts, capacity, model_dim)
        recv_buf = lax.all_to_all(send_buf, 'expert', 0, 2, tiled=True).reshape(loc_experts, expert_size * capacity, model_dim)
        w_gate = lax.all_gather(gate_part, 'data', axis=1, tiled=True)
        w_up = lax.all_gather(up_part, 'data', axis=1, tiled=True)
        w_down = lax.all_gather(down_part, 'data', axis=2, tiled=True)
        act_gate = jnp.einsum('ncm,nmf->ncf', recv_buf, w_gate, preferred_element_type=jnp.float32)
        act_up = jnp.einsum('ncm,nmf->ncf', recv_buf, w_up, preferred_element_type=jnp.float32)
        mid_act = (jax.nn.silu(act_gate) * act_up).astype(jnp.bfloat16)
        expert_out = jnp.einsum('ncf,nfm->ncm', mid_act, w_down, preferred_element_type=jnp.float32).astype(jnp.bfloat16)
        returned = lax.all_to_all(expert_out.reshape(1, loc_experts, expert_size * capacity, model_dim), 'expert', 2, 0, tiled=True)
        mixed_sum = combine_rows(returned.reshape(num_experts * capacity, model_dim), target_rows, gate_loc.reshape(tok_dev, top_k))
        total = flat_hidden.astype(jnp.float32) + mixed_sum
        return total.astype(jnp.bfloat16).reshape(num_seqs, seq_len, model_dim)

    in_specs = (tok_spec, tok_spec, tok_spec, P(None), P(group_axes, None, None), P(None, None, group_axes), P(None), P('expert', 'data', None), P('expert', 'data', None), P('expert', None, 'data'))
    return jax.shard_map(local_step, mesh=mesh, in_specs=in_specs, out_specs=tok_spec, check_vma=False)
```

profile of v0, /device:TPU:0, one launch (start us, length us, event | category | flops | bytes accessed | tf_op | source)
XLA Modules:
  0.0 2911.7 jit_solution(2028090477129068281)
XLA Ops:
  6.5 5.3 copy.38
  11.9 7.6 copy.33
  19.6 0.7 all-gather.12.cloned.1.call-update
  20.9 0.6 iota_compare_fusion.2
  22.8 0.6 fusion.51
  23.4 5.6 fusion.10
  29.0 0.8 fusion.44
  29.8 2.3 reduce-window.6
  33.1 0.6 mul.251
  34.5 0.6 copy-done.9
  35.1 15.7 scatter_custom_fusion
  50.8 0.6 fusion.53
  51.4 0.6 compare_and_fusion.1
  52.0 75.8 %all-gather.8.cloned.1.call-done = bf16[36,64,2304]{1,0,2:T(8,128)(2,1)} async-done(((bf16[36,64,288]{1,0,2:T(8,128)(2,1)}), bf16[36,64,2304]{1,0,2:T(8,128)(2,1)}) %all-gather.8.cloned.1.call-update) | async-done | bytes 10616848 | tf_op jit(solution)/shard_map/all_gather | solution.py:82
  127.8 27.0 copy.39
  154.8 148.9 %all-gather.6.cloned.1.call-done = bf16[2304,108,64]{1,0,2:T(8,128)(2,1)} async-done(((bf16[288,108,64]{1,0,2:T(8,128)(2,1)}), bf16[2304,108,64]{1,0,2:T(8,128)(2,1)}) %all-gather.6.cloned.1.call-update) | async-done | bytes 31850512 | tf_op jit(solution)/shard_map/all_gather | solution.py:81
  303.7 83.6 %fusion.7 = bf16[16,128,108,64]{1,2,3,0:T(8,128)(2,1)} fusion(bf16[2304,108,64]{1,0,2:T(8,128)(2,1)} %all-gather.6.cloned.1.call-done, bf16[16,128,2304]{2,1,0:T(8,128)(2,1)} %param.10, f32[2304]{0:T(1024)S(1)} %copy-done.14, f32[16,128]{1,0:T(8,128)S(1)} %add_rsqrt_fusion), kind=kOutput, calls=%fused_computation.20 | convolution fusion | flops 65262845952 | bytes 69616640 | tf_op jit(solution)/shard_map/uno,ojf->unjf/dot_general | solution.py:36
  387.2 24.6 fusion.52
  411.9 15.6 subtract_convert_fusion.1
  427.5 17.4 pad_maximum_fusion
  444.9 20.7 fusion.4
  465.6 16.3 fusion.3
  481.9 24.0 fusion.16
  505.9 31.8 %multiply_reduce_fusion.1 = (f32[16,128]{1,0:T(8,128)S(1)}, f32[16,128,2304]{2,1,0:T(8,128)S(1)}) fusion(bf16[36,64,2304]{2,1,0:T(8,128)(2,1)} %copy.39, bf16[16,36,64,128]{3,2,1,0:T(8,128)(2,1)} %fusion.16, bf16[16,128,2304]{2,1,0:T(8,128)(2,1)} %param.10), kind=kOutput, calls=%fused_computation.31 | convolution fusion | flops 21771581440 | bytes 48373760 | tf_op jit(solution)/shard_map/slkgd,kgdm->slm/dot_general | solution.py:45
  537.8 6.3 copy-done
  544.1 5.2 fusion.15
  549.3 7.8 concatenate.18
  557.1 48.5 %gather_fusion = bf16[5120,2304]{1,0:T(8,128)(2,1)} fusion(bf16[2049,2304]{1,0:T(8,128)(2,1)} %concatenate.18, s32[5120]{0:T(1024)S(1)} %copy-done.3), kind=kCustom, calls=%fused_computation | custom fusion | bytes 47206400 | tf_op jit(solution)/shard_map/jit(_take)/gather | solution.py:65
  605.6 20.3 broadcast_select_fusion.1
  625.9 8.2 all-to-all-start
  634.7 255.1 %all-to-all-done = bf16[4,2,640,2304]{3,2,1,0:T(8,128)(2,1)} async-done(((bf16[4,2,640,2304]{3,2,1,0:T(8,128)(2,1)}), bf16[4,2,640,2304]{3,2,1,0:T(8,128)(2,1)}, u32[]{:S(2)}, u32[]{:S(2)}) %all-to-all-start) | async-done | bytes 23592992 | tf_op jit(solution)/shard_map/all_to_all | solution.py:94
  889.9 19.8 copy.45
  909.7 4.6 all-gather.12.cloned.1.call-done
  914.3 157.9 %fusion.56 = f32[2,2560,5760]{2,1,0:T(8,128)} fusion(bf16[2,2560,2304]{2,1,0:T(8,128)(2,1)} %bitcast.113, bf16[2,2304,5760]{2,1,0:T(8,128)(2,1)} %all-gather.12.cloned.1.call-done), kind=kOutput, calls=%fused_computation.95 | convolution fusion | flops 135895449600 | bytes 194641920 | tf_op jit(solution)/shard_map/ncm,nmf->ncf/dot_general | solution.py:99
  1072.2 452.5 %all-gather.10.cloned.1.call-done = bf16[2,2304,5760]{2,1,0:T(8,128)(2,1)} async-done(((bf16[2,1152,5760]{2,1,0:T(8,128)(2,1)}), bf16[2,2304,5760]{2,1,0:T(8,128)(2,1)}) %all-gather.10.cloned.1.call-update) | async-done | bytes 53084176 | tf_op jit(solution)/shard_map/all_gather | solution.py:95
  1524.7 180.6 %multiply_convert_fusion.8 = bf16[2,2560,5760]{2,1,0:T(8,128)(2,1)} fusion(f32[2,2560,5760]{2,1,0:T(8,128)} %fusion.56, bf16[2,2560,2304]{2,1,0:T(8,128)(2,1)} %bitcast.114, bf16[2,2304,5760]{2,1,0:T(8,128)(2,1)} %all-gather.10.cloned.1.call-done), kind=kOutput, calls=%fused_computation.3.clone.clone.clone.clone.clone.clone.1 | convolution fusion | flops 136072396800 | bytes 253624320 | tf_op jit(solution)/shard_map/ncm,nmf->ncf/dot_general | solution.py:98
  1705.3 427.5 %all-gather.14.cloned.1.call-done = bf16[2,5760,2304]{2,1,0:T(8,128)(2,1)} async-done(((bf16[2,5760,1152]{2,1,0:T(8,128)(2,1)}), bf16[2,5760,2304]{2,1,0:T(8,128)(2,1)}) %all-gather.14.cloned.1.call-update) | async-done | bytes 53084176 | tf_op jit(solution)/shard_map/all_gather | solution.py:97
  2132.8 152.5 %fusion.6 = bf16[1,2,2560,2304]{3,2,1,0:T(8,128)(2,1)} fusion(bf16[2,5760,2304]{2,1,0:T(8,128)(2,1)} %all-gather.14.cloned.1.call-done, bf16[2,2560,5760]{2,1,0:T(8,128)(2,1)} %multiply_convert_fusion.8), kind=kOutput, calls=%fused_computation.19 | convolution fusion | flops 135907246080 | bytes 135659520 | tf_op jit(solution)/shard_map/ncf,nfm->ncm/dot_general | solution.py:101
  2285.3 43.1 %copy.46 = bf16[1,2,2560,2304]{3,1,0,2:T(2,128)(2,1)} copy(bf16[1,2,2560,2304]{3,2,1,0:T(8,128)(2,1)} %fusion.6) | data formatting | bytes 47185920 | tf_op jit(solution)/shard_map/reshape | solution.py:102
  2328.5 8.7 all-to-all-start.1
  2337.1 1.0 reduce_sum.54
  2339.3 253.5 %all-to-all-done.1 = bf16[1,2,2560,2304]{3,1,0,2:T(2,128)(2,1)} async-done(((bf16[1,2,2560,2304]{3,1,0,2:T(2,128)(2,1)}), bf16[1,2,2560,2304]{3,1,0,2:T(2,128)(2,1)}, u32[]{:S(2)}, u32[]{:S(2)}) %all-to-all-start.1) | async-done | bytes 23592992 | tf_op jit(solution)/shard_map/all_to_all | solution.py:102
  2592.8 14.8 copy.47
  2607.6 9.7 concatenate.19
  2617.3 45.9 %gather_fusion.1 = bf16[4096,2304]{1,0:T(8,128)(2,1)} fusion(bf16[5121,2304]{1,0:T(8,128)(2,1)} %concatenate.19, s32[4096]{0:T(1024)S(1)} %broadcast_clamp_fusion), kind=kCustom, calls=%fused_computation.1 | custom fusion | bytes 37765120 | tf_op jit(solution)/shard_map/jit(_take)/gather | solution.py:71
  2663.2 36.3 %gather.15 = bf16[2048,2,2304]{2,1,0:T(2,128)(2,1)} reshape(bf16[4096,2304]{1,0:T(8,128)(2,1)} %gather_fusion.1) | data formatting | bytes 37748736 | tf_op jit(solution)/shard_map/jit(_take)/gather | solution.py:71
  2699.6 195.5 %multiply_reduce_fusion = f32[2048,2304]{1,0:T(8,128)S(1)} fusion(bf16[2048,2,2304]{2,1,0:T(2,128)(2,1)} %gather.15, pred[2048,2]{1,0:T(8,128)(4,1)S(1)} %compare_and_fusion, f32[2048,2]{1,0:T(8,128)S(1)} %copy.49), kind=kLoop, calls=%fused_computation.8 | loop fusion | flops 33030144 | bytes 37769216 | tf_op jit(solution)/shard_map/reduce_sum | solution.py:72
  2895.0 10.0 add_convert_fusion
  (56 shorter events, 5.5 us)
Async XLA Ops:
  6.5 121.3 %all-gather.8.cloned.1.call-start = ((), (), s32[]{:S(2)}) async-start(), calls=%async_computation.3 | async-start | bytes 26542080 | tf_op jit(solution)/shard_map/all_gather | solution.py:82
  11.9 291.8 %all-gather.6.cloned.1.call-start = ((), (), s32[]{:S(2)}) async-start(), calls=%async_computation.2 | async-start | bytes 42467328 | tf_op jit(solution)/shard_map/all_gather | solution.py:81
  19.5 894.7 %all-gather.12.cloned.1.call-start = ((), (), s32[]{:S(2)}) async-start(), calls=%async_computation.5 | async-start | bytes 79626240 | tf_op jit(solution)/shard_map/all_gather | solution.py:96
  20.3 1.2 copy-start.4
  20.3 1504.4 %all-gather.10.cloned.1.call-start = ((), (), s32[]{:S(2)}) async-start(), calls=%async_computation.4 | async-start | bytes 79626240 | tf_op jit(solution)/shard_map/all_gather | solution.py:95
  29.0 274.7 %copy-start.14 = (f32[2304]{0:T(1024)S(1)}, f32[2304]{0:T(1024)}, u32[]{:S(2)}) copy-start(f32[2304]{0:T(1024)} %param.13) | copy-start | bytes 27652
  33.8 0.6 copy-start.1
  34.5 0.6 copy-start.9
  387.2 24.6 copy-start.7
  387.2 24.6 copy-start.8
  427.5 17.4 copy-start.6
  505.9 38.2 %copy-start.13 = (f32[2304]{0:T(1024)S(1)}, f32[2304]{0:T(1024)}, u32[]{:S(2)}) copy-start(f32[2304]{0:T(1024)} %param.16) | copy-start | bytes 27652
  537.8 6.4 copy-start
  544.1 13.0 copy-start.3
  557.1 48.5 %copy-start.11 = (pred[4,2,640]{2,1,0:T(4,128)(4,1)S(1)}, pred[4,2,640]{2,1,0:T(4,128)(4,1)}, u32[]{:S(2)}) copy-start(pred[4,2,640]{2,1,0:T(4,128)(4,1)} %compare_and_fusion.1) | copy-start | bytes 15364
  625.9 263.9 %all-to-all-start = ((bf16[4,2,640,2304]{3,2,1,0:T(8,128)(2,1)}), bf16[4,2,640,2304]{3,2,1,0:T(8,128)(2,1)}, u32[]{:S(2)}, u32[]{:S(2)}) async-start(bf16[4,2,640,2304]{3,2,1,0:T(8,128)(2,1)} %broadcast_select_fusion.1), calls=%async_computation | async-start | bytes 47185920 | tf_op jit(solution)/shard_map/all_to_all | solution.py:94
  634.1 1498.7 %all-gather.14.cloned.1.call-start = ((), (), s32[]{:S(2)}) async-start(), calls=%async_computation.6 | async-start | bytes 79626240 | tf_op jit(solution)/shard_map/all_gather | solution.py:97
  2328.4 8.7 copy-start.2
  2328.4 9.7 copy-start.5
  2328.4 10.1 copy-start.12
  2328.4 10.5 copy-start.10
  2328.5 264.4 %all-to-all-start.1 = ((bf16[1,2,2560,2304]{3,1,0,2:T(2,128)(2,1)}), bf16[1,2,2560,2304]{3,1,0,2:T(2,128)(2,1)}, u32[]{:S(2)}, u32[]{:S(2)}) async-start(bf16[1,2,2560,2304]{3,1,0,2:T(2,128)(2,1)} %copy.46), calls=%async_computation.1 | async-start | bytes 47185920 | tf_op jit(solution)/shard_map/all_to_all | solution.py:102
Sparse Core Ops, SparseCore 0:
  12.0 115.7 all-gather.7
  129.7 173.9 all-gather.5
  305.2 608.9 all-gather.11
  915.6 608.9 all-gather.9
  1526.0 606.7 all-gather.13
where the time goes:
time: 2920 us; the launch traced here: 2910 us
  waiting for transfers between devices  1620 us (55%)
  matrix products  651 us (22%)
  other arithmetic  317 us (11%)
  local copies, waits for them, and re-layouts  293 us (10%)
    all_gather x1, waiting for transfers between devices, local_step(): w_gate = lax.all_gather(gate_part, 'data', axis=1, tiled=True)  452 us
    all_gather x1, waiting for transfers between devices, local_step(): w_down = lax.all_gather(down_part, 'data', axis=2, tiled=True)  428 us
    all_to_all x1, waiting for transfers between devices, local_step(): lax.all_to_all(send_buf, 'expert', 0, 2, tiled=True)  255 us
    all_to_all x1, waiting for transfers between devices, local_step(): lax.all_to_all(expert_out.reshape(1, loc_experts, expert_size * capacity,...  253 us
    reduce_sum x1, other arithmetic, combine_rows(): return jnp.sum(picked.astype(jnp.float32) * gate_rows[:, :, None], axis=1)  195 us
    dot_general x1, matrix products, local_step(): jnp.einsum('ncm,nmf->ncf', recv_buf, w_gate, preferred_element_type=jnp.f...  181 us
    dot_general x1, matrix products, local_step(): jnp.einsum('ncm,nmf->ncf', recv_buf, w_up, preferred_element_type=jnp.flo...  158 us
    dot_general x1, matrix products, local_step(): jnp.einsum('ncf,nfm->ncm', mid_act, w_down, preferred_element_type=jnp.fl...  152 us
  transfers between devices with their start and end apart: 7, of which 7 were waited for; matrix products, arithmetic and copies ran while one was open for 25% of the time, Pallas kernels for 0%

commit v1 on v0

v1 whole, which is shorter than its diff:
```python
import functools

import jax
import jax.numpy as jnp
from jax import lax
from jax.experimental import pallas as pl
from jax.experimental.pallas import tpu as pltpu
from jax.sharding import PartitionSpec as P

NORM_EPS = 1e-6
ROPE_BASE = 10000.0


def rms_scale(tok_rows, gain):
    rows_f32 = tok_rows.astype(jnp.float32)
    inv_rms = lax.rsqrt(jnp.mean(rows_f32 * rows_f32, axis=-1, keepdims=True) + NORM_EPS)
    return (rows_f32 * inv_rms * gain).astype(jnp.bfloat16)


def rope_apply(head_vals):
    seq_len, head_dim = head_vals.shape[1], head_vals.shape[-1]
    half_dim = head_dim // 2
    inv_freq = ROPE_BASE ** (-jnp.arange(half_dim, dtype=jnp.float32) * 2.0 / head_dim)
    angles = jnp.arange(seq_len, dtype=jnp.float32)[:, None] * inv_freq[None, :]
    cos_b = jnp.cos(angles)[None, :, None, :]
    sin_b = jnp.sin(angles)[None, :, None, :]
    vals_f32 = head_vals.astype(jnp.float32)
    low_half = vals_f32[..., :half_dim]
    high_half = vals_f32[..., half_dim:]
    return jnp.concatenate([low_half * cos_b - high_half * sin_b, high_half * cos_b + low_half * sin_b], axis=-1).astype(jnp.bfloat16)


def attention_block(seqs, attn_gain, w_qkv, w_out_t, num_heads, head_dim):
    num_seqs, seq_len, model_dim = seqs.shape
    normed = rms_scale(seqs, attn_gain).reshape(num_seqs * seq_len, model_dim)
    qkv = jnp.dot(normed, w_qkv, preferred_element_type=jnp.float32).astype(jnp.bfloat16)
    qkv_all = qkv.reshape(num_seqs, seq_len, -1, head_dim)
    kv_heads = qkv_all.shape[2] - 2 * num_heads
    queries = rope_apply(qkv_all[:, :, :num_heads])
    keys_rot = rope_apply(qkv_all[:, :, num_heads:num_heads + kv_heads])
    values = qkv_all[:, :, num_heads + kv_heads:]
    scores = jnp.einsum('slkd,smkd->sklm', queries, keys_rot, preferred_element_type=jnp.float32) * (head_dim ** -0.5)
    causal = lax.broadcasted_iota(jnp.int32, (seq_len, seq_len), 0) >= lax.broadcasted_iota(jnp.int32, (seq_len, seq_len), 1)
    attn_probs = jax.nn.softmax(jnp.where(causal, scores, -1e30), axis=-1).astype(jnp.bfloat16)
    mixed = jnp.einsum('sklm,smkd->slkd', attn_probs, values, preferred_element_type=jnp.float32).astype(jnp.bfloat16)
    attn_proj = lax.dot_general(mixed.reshape(num_seqs * seq_len, num_heads * head_dim), w_out_t, (((1,), (1,)), ((), ())), preferred_element_type=jnp.float32)
    return (seqs.reshape(num_seqs * seq_len, model_dim).astype(jnp.float32) + attn_proj).astype(jnp.bfloat16)


def capacity_of(tok_dev, top_k, num_experts):
    return 8 * ((5 * top_k * tok_dev + 32 * num_experts - 1) // (32 * num_experts))


def slots_of(flat_ids, num_experts):
    onehot = (flat_ids[:, None] == jnp.arange(num_experts, dtype=jnp.int32)[None, :]).astype(jnp.int32)
    earlier = jnp.cumsum(onehot, axis=0) - onehot
    return jnp.sum(earlier * onehot, axis=1)


def tile_of(size, most):
    return max(t for t in range(128, most + 1, 128) if size % t == 0)


def up_kernel(ids_ref, z_a, z_b, wg_a, wg_b, wu_a, wu_b, mid_ref):
    ff = mid_ref.shape[1]
    w_a = jnp.concatenate([wg_a[0], wu_a[0]], axis=1)
    w_b = jnp.concatenate([wg_b[0], wu_b[0]], axis=1)
    w = jnp.concatenate([w_a, w_b], axis=0)
    rows = mid_ref.shape[0]
    start = pl.multiple_of(pl.program_id(1) * rows, rows)
    z = jnp.concatenate([z_a[pl.ds(start, rows), :], z_b[pl.ds(start, rows), :]], axis=1)
    acc = jnp.dot(z, w, preferred_element_type=jnp.float32)
    act_gate = acc[:, :ff]
    mid_ref[...] = (act_gate * jax.nn.sigmoid(act_gate) * acc[:, ff:]).astype(mid_ref.dtype)


def expert_up(ids, z, wg_own, wg_got, wu_own, wu_got):
    rows, model_dim = z.shape
    half = model_dim // 2
    ff_dim = wg_own.shape[2]
    ff = tile_of(ff_dim, 384)
    rb = tile_of(rows, 1280)
    own = pl.BlockSpec((1, half, ff), lambda j, i, s: (s[0], 0, j))
    got = pl.BlockSpec((1, half, ff), lambda j, i, s: (1 - s[0], 0, j))
    once = pl.Buffered(buffer_count=1)
    return pl.pallas_call(
        up_kernel,
        grid_spec=pltpu.PrefetchScalarGridSpec(
            num_scalar_prefetch=1,
            grid=(ff_dim // ff, rows // rb),
            in_specs=[
                pl.BlockSpec((rows, half), lambda j, i, s: (0, s[0]), pipeline_mode=once),
                pl.BlockSpec((rows, half), lambda j, i, s: (0, 1 - s[0]), pipeline_mode=once),
                own, got, own, got,
            ],
            out_specs=pl.BlockSpec((rb, ff), lambda j, i, s: (i, j)),
        ),
        out_shape=jax.ShapeDtypeStruct((rows, ff_dim), jnp.bfloat16),
        compiler_params=pltpu.CompilerParams(dimension_semantics=("arbitrary", "arbitrary"), vmem_limit_bytes=60 * 2**20),
        cost_estimate=pl.CostEstimate(flops=4 * rows * model_dim * ff_dim, bytes_accessed=2 * (rows * model_dim + 2 * model_dim * ff_dim + rows * ff_dim), transcendentals=rows * ff_dim),
        name="expert_up",
    )(ids, z, z, wg_own, wg_got, wu_own, wu_got)


def down_kernel(ids_ref, mid_ref, w_a, w_b, out_ref):
    half = w_a.shape[2]
    w = jnp.concatenate([w_a[0], w_b[0]], axis=1)
    acc = jnp.dot(mid_ref[...], w, preferred_element_type=jnp.float32)
    first = ids_ref[0] == 0
    own, got = acc[:, :half], acc[:, half:]
    out_ref[:, :half] = jnp.where(first, own, got).astype(out_ref.dtype)
    out_ref[:, half:] = jnp.where(first, got, own).astype(out_ref.dtype)


def expert_down(ids, mid, w_own, w_got):
    rows, ff_dim = mid.shape
    half = w_own.shape[2]
    rb = tile_of(rows, 320) if rows % 256 else 256
    once = pl.Buffered(buffer_count=1)
    return pl.pallas_call(
        down_kernel,
        grid_spec=pltpu.PrefetchScalarGridSpec(
            num_scalar_prefetch=1,
            grid=(rows // rb,),
            in_specs=[
                pl.BlockSpec((rb, ff_dim), lambda i, s: (i, 0)),
                pl.BlockSpec((1, ff_dim, half), lambda i, s: (s[0], 0, 0), pipeline_mode=once),
                pl.BlockSpec((1, ff_dim, half), lambda i, s: (1 - s[0], 0, 0), pipeline_mode=once),
            ],
            out_specs=pl.BlockSpec((rb, 2 * half), lambda i, s: (i, 0)),
        ),
        out_shape=jax.ShapeDtypeStruct((rows, 2 * half), jnp.bfloat16),
        compiler_params=pltpu.CompilerParams(dimension_semantics=("arbitrary",), vmem_limit_bytes=60 * 2**20),
        cost_estimate=pl.CostEstimate(flops=4 * rows * half * ff_dim, bytes_accessed=2 * (2 * rows * half + 2 * half * ff_dim + rows * ff_dim), transcendentals=0),
        name="expert_down",
    )(ids, mid, w_own, w_got)


def solution(mesh):
    tok_spec = P(('rep', 'expert', 'data'), None, None)
    group_axes = ('data', 'expert')
    token_axes = ('expert', 'data')
    num_experts = mesh.shape['expert'] * mesh.shape['data']

    def local_step(x_loc, idx_loc, gate_loc, attn_gain, qkv_part, out_part, moe_gain, gate_part, up_part, down_part):
        num_seqs, seq_len, model_dim = x_loc.shape
        num_heads, head_dim = out_part.shape[0], out_part.shape[1]
        tok_dev = num_seqs * seq_len
        top_k = idx_loc.shape[-1]
        capacity = capacity_of(tok_dev, top_k, num_experts)
        mine = lax.axis_index('data')
        ids = jnp.stack([mine]).astype(jnp.int32)

        w_qkv = lax.all_gather(qkv_part.reshape(qkv_part.shape[0], -1), group_axes, axis=0, tiled=True)
        w_out_t = lax.all_gather(out_part.reshape(num_heads * head_dim, -1).T, group_axes, axis=0, tiled=True)

        def swap(part):
            return lax.all_gather(lax.dynamic_index_in_dim(part, 1 - mine, 0, keepdims=False), 'data')

        got_gate, got_up, got_down = swap(gate_part), swap(up_part), swap(down_part)

        flat_ids = idx_loc.reshape(tok_dev * top_k)
        slot_pos = slots_of(flat_ids, num_experts)
        kept = slot_pos < capacity
        target = flat_ids * capacity + slot_pos
        source = jnp.zeros((num_experts * capacity,), jnp.int32)
        source = source.at[jnp.where(kept, target, num_experts * capacity)].set(jnp.arange(tok_dev * top_k, dtype=jnp.int32) // top_k, mode='drop', unique_indices=False)

        hidden = attention_block(x_loc, attn_gain, w_qkv, w_out_t, num_heads, head_dim)
        normed = rms_scale(hidden, moe_gain)
        send = normed.at[source].get(mode='promise_in_bounds')
        rows = lax.all_to_all(send.reshape(num_experts, capacity, model_dim), token_axes, 0, 0, tiled=True)
        mid = expert_up(ids, rows.reshape(num_experts * capacity, model_dim), gate_part, got_gate, up_part, got_up)
        outs = expert_down(ids, mid, down_part, got_down)
        back = lax.all_to_all(outs.reshape(num_experts, capacity, model_dim), token_axes, 0, 0, tiled=True).reshape(num_experts * capacity, model_dim)
        pick = jnp.where(kept, target, 0).reshape(tok_dev, top_k)
        kept = kept.reshape(tok_dev, top_k)
        gates = gate_loc.reshape(tok_dev, top_k)
        mixed = None
        for k in range(top_k):
            got = back.at[pick[:, k]].get(mode='promise_in_bounds').astype(jnp.float32)
            term = jnp.where(kept[:, k, None], got * gates[:, k, None], 0.0)
            mixed = term if mixed is None else mixed + term
        total = hidden.astype(jnp.float32) + mixed
        return total.astype(jnp.bfloat16).reshape(num_seqs, seq_len, model_dim)

    in_specs = (tok_spec, tok_spec, tok_spec, P(None), P(group_axes, None, None), P(None, None, group_axes), P(None), P('expert', 'data', None), P('expert', 'data', None), P('expert', None, 'data'))
    return jax.shard_map(local_step, mesh=mesh, in_specs=in_specs, out_specs=tok_spec, check_vma=False)
```

time: 2920 us -> 1920 us (0.66)
  waiting for transfers between devices: 1620 us -> 789 us
  matrix products: 651 us -> 153 us
  Pallas kernels: 0 us -> 455 us
  other arithmetic: 317 us -> 136 us
  local copies, waits for them, and re-layouts: 293 us -> 356 us
    all_gather x5, waiting for transfers between devices: 1110 us -> 536 us  [the longest x3 448 us: swap(): lax.all_gather(lax.dynamic_index_in_dim(part, 1 - mine, 0, keepdims=False...]
    dot_general x7 -> x4, matrix products: 651 us -> 153 us  [the longest x1 74.6 us: attention_block(): jnp.dot(normed, w_qkv, preferred_element_type=jnp.float32)]
    pallas_call x0 -> x2, Pallas kernels: none -> 455 us  [the longest x1 301 us: expert_up(): pl.pallas_call(up_kernel, grid_spec=pltpu.PrefetchScalarGridSpec(num_scal...]
    all_to_all x2, waiting for transfers between devices: 509 us -> 253 us  [the longest x1 253 us: local_step(): lax.all_to_all(outs.reshape(num_experts, capacity, model_dim), token_axes...]
    reduce_sum x3 -> x1, other arithmetic: 212 us -> 0.11 us  [slots_of(): return jnp.sum(earlier * onehot, axis=1)]
    slice x2 -> x4, local copies, waits for them, and re-layouts: 0.32 us -> 45.4 us  [the longest x1 44.2 us: attention_block(): values = qkv_all[:, :, num_heads + kv_heads:]]
    sub x0 -> x1, other arithmetic: none -> 42.8 us  [attention_block(): jax.nn.softmax(jnp.where(causal, scores, -1e+30), axis=-1)]
    all_to_all x2 -> x0, local copies, waits for them, and re-layouts: 34.6 us -> none  [the longest x1 19.8 us: local_step(): lax.all_to_all(send_buf, 'expert', 0, 2, tiled=True)]
  transfers between devices with their start and end apart: 7 -> 7, of which waited for: 7 -> 4; matrix products, arithmetic and copies ran while one was open for 25% -> 29% of each run, Pallas kernels for 0% -> 16%
where the time goes in v1:
time: 1920 us; the launch traced here: 1910 us
  waiting for transfers between devices  789 us (41%)
  Pallas kernels  455 us (24%)
  local copies, waits for them, and re-layouts  356 us (19%)
  matrix products  153 us (8%)
  other arithmetic  136 us (7%)
    all_gather x3, waiting for transfers between devices, swap(): lax.all_gather(lax.dynamic_index_in_dim(part, 1 - mine, 0, keepdims=False...  448 us
    pallas_call x1, Pallas kernels, expert_up(): pl.pallas_call(up_kernel, grid_spec=pltpu.PrefetchScalarGridSpec(num_scal...  301 us
    all_to_all x1, waiting for transfers between devices, local_step(): lax.all_to_all(outs.reshape(num_experts, capacity, model_dim), token_axes...  253 us
    pallas_call x1, Pallas kernels, expert_down(): pl.pallas_call(down_kernel, grid_spec=pltpu.PrefetchScalarGridSpec(num_sc...  154 us
    all_gather x1, waiting for transfers between devices, local_step(): lax.all_gather(qkv_part.reshape(qkv_part.shape[0], -1), group_axes, axis=...  88 us
    dot_general x1, matrix products, attention_block(): jnp.dot(normed, w_qkv, preferred_element_type=jnp.float32)  74.6 us
    reshape x1, local copies, waits for them, and re-layouts, attention_block(): qkv_all = qkv.reshape(num_seqs, seq_len, -1, head_dim)  65.8 us
    gather x2, local copies, waits for them, and re-layouts, local_step(): got = back.at[pick[:, k]].get(mode='promise_in_bounds').astype(jnp.float32)  57.9 us
  transfers between devices with their start and end apart: 7, of which 4 were waited for; matrix products, arithmetic and copies ran while one was open for 29% of the time, Pallas kernels for 16%

profile of v1, /device:TPU:0, one launch (start us, length us, event | category | flops | bytes accessed | tf_op | source)
XLA Modules:
  0.0 1912.6 jit_solution(16198082589407516200)
XLA Ops:
  6.5 9.4 copy.43
  16.0 6.7 copy.44
  22.8 1.7 copy.51
  24.5 10.8 constant_dynamic-slice_fusion.2
  35.4 10.8 constant_dynamic-slice_fusion.1
  46.3 0.6 iota_compare_fusion.2
  47.3 0.5 eq.29
  47.7 0.5 eq.25
  48.2 0.6 fusion.40
  48.8 5.6 multiply_reduce_fusion
  54.4 0.8 fusion.33
  55.2 2.3 reduce-window.6
  58.1 0.4 copy.54
  58.5 0.6 mul.247
  59.2 0.6 copy-done.1
  59.9 15.5 scatter_custom_fusion
  75.4 0.6 fusion.29
  76.0 9.6 multiply_convert_fusion
  85.7 88.0 %all-gather.6.cloned.1.call-done = bf16[2304,6912]{1,0:T(8,128)(2,1)} async-done(((bf16[288,6912]{1,0:T(8,128)(2,1)}), bf16[2304,6912]{1,0:T(8,128)(2,1)}) %all-gather.6.cloned.1.call-update) | async-done | bytes 31850512 | tf_op jit(solution)/shard_map/all_gather | solution.py:154
  173.7 74.6 %convolution_convert_fusion = bf16[2048,6912]{1,0:T(8,128)(2,1)} fusion(bf16[2048,2304]{1,0:T(8,128)(2,1)} %bitcast.59, bf16[2304,6912]{1,0:T(8,128)(2,1)} %all-gather.6.cloned.1.call-done), kind=kOutput, calls=%fused_computation.12 | convolution fusion | flops 65243971584 | bytes 69599232 | tf_op jit(solution)/shard_map/dot_general | solution.py:36
  248.3 65.8 %reshape.207 = bf16[16,128,108,64]{3,2,1,0:T(8,128)(2,1)} reshape(bf16[2048,6912]{1,0:T(8,128)(2,1)} %convolution_convert_fusion) | data formatting | bytes 56623104 | tf_op jit(solution)/shard_map/reshape | solution.py:37
  314.1 44.2 %fusion.41 = (bf16[16,128,36,64]{3,2,1,0:T(8,128)(2,1)}, bf16[16,128,36,64]{3,2,1,0:T(8,128)(2,1)}, bf16[16,128,36,64]{3,2,1,0:T(8,128)(2,1)}) fusion(bf16[16,128,108,64]{3,2,1,0:T(8,128)(2,1)} %reshape.207), kind=kLoop, calls=%fused_computation.87 | loop fusion | bytes 56623104 | tf_op jit(solution)/shard_map/slice | solution.py:41
  358.3 20.7 %copy.62 = bf16[16,128,36,64]{1,3,2,0:T(8,128)(2,1)} copy(bf16[16,128,36,64]{3,2,1,0:T(8,128)(2,1)} %get-tuple-element.10) | data formatting | bytes 18874368
  379.0 12.6 convert_element_type.63
  391.6 21.1 %copy.63 = bf16[16,128,36,64]{1,3,2,0:T(8,128)(2,1)} copy(bf16[16,128,36,64]{3,2,1,0:T(8,128)(2,1)} %get-tuple-element.11) | data formatting | bytes 18874368
  412.6 12.6 convert_element_type.64
  425.2 21.2 %subtract_convert_fusion = (bf16[16,128,36,32]{1,3,2,0:T(8,128)(2,1)}, bf16[16,128,36,32]{1,3,2,0:T(8,128)(2,1)}, bf16[16,128,36,32]{1,3,2,0:T(8,128)(2,1)}, bf16[16,128,36,32]{1,3,2,0:T(8,128)(2,1)}) fusion(f32[16,128,36,64]{1,3,2,0:T(8,128)} %convert_element_type.64, f32[128,32]{0,1:T(8,128)S(1)} %copy-done.7, f32[128,32]{0,1:T(8,128)S(1)} %copy-done.6, ...), kind=kLoop, calls=%fused_computation.37 | loop fusion | flops 37748736 | bytes 56655872 | tf_op jit(solution)/shard_map/convert.1
  446.4 19.1 fusion.14
  465.5 42.8 %fusion.43 = (f32[16,36,128]{2,1,0:T(8,128)S(1)}, f32[16,36,128,128]{2,3,1,0:T(8,128)}) fusion(f32[16,36,128,128]{2,3,1,0:T(8,128)} %fusion.14, pred[128,128]{0,1:T(8,128)(4,1)S(1)} %copy-done.9), kind=kOutput, calls=%fused_computation.89 | output fusion | flops 56623232 | bytes 75808768 | tf_op jit(solution)/shard_map/sub | solution.py:44
  508.4 23.5 %convert_bitcast_fusion = bf16[16,128,36,64]{1,3,2,0:T(8,128)(2,1)} fusion(f32[16,36,128,128]{2,3,1,0:T(8,128)} %get-tuple-element.25, f32[16,36,128]{2,1,0:T(8,128)S(1)} %get-tuple-element.24, bf16[16,128,36,64]{3,2,1,0:T(8,128)(2,1)} %get-tuple-element.9), kind=kOutput, calls=%fused_computation.35 | convolution fusion | flops 1231552512 | bytes 56918016 | tf_op jit(solution)/shard_map/sklm,smkd->slkd/dot_general | solution.py:45
  531.8 26.0 %copy.50 = bf16[16,128,36,64]{1,0,3,2:T(8,128)(2,1)} copy(bf16[16,128,36,64]{1,3,2,0:T(8,128)(2,1)} %convert_bitcast_fusion) | data formatting | bytes 18874368 | tf_op jit(solution)/shard_map/convert_element_type | solution.py:45
  557.8 35.4 %fusion.2 = (f32[2048]{0:T(1024)S(1)}, bf16[2048,2304]{1,0:T(8,128)(2,1)}) fusion(bf16[2304,2304]{1,0:T(8,128)(2,1)} %all-gather.8.cloned.1.call-done, bf16[288,8,16,128]{3,2,1,0:T(8,128)(2,1)} %bitcast.58, bf16[16,128,2304]{2,1,0:T(8,128)(2,1)} %param.10), kind=kOutput, calls=%fused_computation.13 | convolution fusion | flops 21771581440 | bytes 38936576 | tf_op jit(solution)/shard_map/dot_general | solution.py:46
  593.2 9.5 fusion.4
  602.7 48.4 %gather_fusion = bf16[5120,2304]{1,0:T(8,128)(2,1)} fusion(bf16[2048,2304]{1,0:T(8,128)(2,1)} %fusion.4, s32[5120]{0:T(1024)S(1)} %copy-done.3), kind=kCustom, calls=%fused_computation | custom fusion | bytes 47206400 | tf_op jit(solution)/shard_map/gather | solution.py:171
  651.2 5.1 all-to-all-start
  656.3 10.9 constant_dynamic-slice_fusion
  667.3 438.7 %all-gather.12.cloned.1.call-done.wu_b = bf16[2,1152,5760]{2,1,0:T(8,128)(2,1)} async-done(((bf16[1,1152,5760]{2,1,0:T(8,128)(2,1)}), bf16[2,1152,5760]{2,1,0:T(8,128)(2,1)}) %all-gather.12.cloned.1.call-update) | async-done | bytes 26542096 | tf_op jit(solution)/shard_map/all_gather | solution.py:158
  1106.0 300.6 %expert_up.1.mid_ref = bf16[5120,5760]{1,0:T(8,128)(2,1)} custom-call(s32[1]{0:T(128)} %bitcast.7.ids_ref, bf16[5120,2304]{1,0:T(8,128)(2,1)} %bitcast.11.z_a.z_b, bf16[5120,2304]{1,0:T(8,128)(2,1)} %bitcast.11.z_a.z_b, bf16[2,1152,5760]{2,1,0:T(8,128)(2,1)} %wg_a.1, bf16[2,1152,5760]{2,1,0:T(8,128)(2,1)} %all-gather.10.cloned.1.call-done.wg_b, ...), custom_call_target="tpu_custom_call" | custom-call | flops 271790899200 | bytes 135659520 | tf_op jit(solution)/shard_map/expert_up/pallas_call | solution.py:86
  1406.5 9.4 all-gather.14.cloned.1.call-done.w_b
  1415.9 154.3 %expert_down.1 = bf16[5120,2304]{1,0:T(8,128)(2,1)} custom-call(s32[1]{0:T(128)} %bitcast.7.ids_ref, bf16[5120,5760]{1,0:T(8,128)(2,1)} %expert_up.1.mid_ref, bf16[2,5760,1152]{2,1,0:T(8,128)(2,1)} %w_a.1, bf16[2,5760,1152]{2,1,0:T(8,128)(2,1)} %all-gather.14.cloned.1.call-done.w_b), custom_call_target="tpu_custom_call" | custom-call | flops 135895449600 | bytes 109117440 | tf_op jit(solution)/shard_map/expert_down/pallas_call | solution.py:120
  1570.2 5.4 all-to-all-start.1
  1575.6 1.0 reduce_sum.43
  1577.2 0.9 slice_reduce_fusion.1
  1578.2 0.9 fusion.23
  1579.2 252.6 %all-to-all-done.1 = bf16[8,640,2304]{2,1,0:T(8,128)(2,1)} async-done(((bf16[8,640,2304]{2,1,0:T(8,128)(2,1)}), bf16[8,640,2304]{2,1,0:T(8,128)(2,1)}, u32[]{:S(2)}, u32[]{:S(2)}) %all-to-all-start.1) | async-done | bytes 23592992 | tf_op jit(solution)/shard_map/all_to_all | solution.py:175
  1831.8 29.0 %gather_fusion.1 = bf16[2048,2304]{1,0:T(8,128)(2,1)} fusion(bf16[5120,2304]{1,0:T(8,128)(2,1)} %bitcast.13, s32[2048]{0:T(1024)S(1)} %get-tuple-element.29), kind=kCustom, calls=%fused_computation.1 | custom fusion | bytes 18882560 | tf_op jit(solution)/shard_map/gather | solution.py:181
  1860.7 29.0 %gather_fusion.2 = bf16[2048,2304]{1,0:T(8,128)(2,1)} fusion(bf16[5120,2304]{1,0:T(8,128)(2,1)} %bitcast.13, s32[2048]{0:T(1024)S(1)} %get-tuple-element.28), kind=kCustom, calls=%fused_computation.2 | custom fusion | bytes 18882560 | tf_op jit(solution)/shard_map/gather | solution.py:181
  1889.7 16.0 fusion.5
  (52 shorter events, 2.1 us)
Async XLA Ops:
  6.5 16.2 copy-start
  6.5 167.2 %all-gather.6.cloned.1.call-start = ((), (), s32[]{:S(2)}) async-start(), calls=%async_computation.2 | async-start | bytes 35831808 | tf_op jit(solution)/shard_map/all_gather | solution.py:154
  22.7 535.1 %all-gather.8.cloned.1.call-start = ((), (), s32[]{:S(2)}) async-start(), calls=%async_computation.3 | async-start | bytes 11943936 | tf_op jit(solution)/shard_map/all_gather | solution.py:155
  24.5 642.8 %all-gather.10.cloned.1.call-start = ((), (), s32[]{:S(2)}) async-start(), calls=%async_computation.4 | async-start | bytes 39813120 | tf_op jit(solution)/shard_map/all_gather | solution.py:158
  35.4 11.5 copy-start.4
  35.4 1070.6 %all-gather.12.cloned.1.call-start = ((), (), s32[]{:S(2)}) async-start(), calls=%async_computation.5 | async-start | bytes 39813120 | tf_op jit(solution)/shard_map/all_gather | solution.py:158
  46.2 29.8 %copy-start.10 = (f32[2304]{0:T(1024)S(1)}, f32[2304]{0:T(1024)}, u32[]{:S(2)}) copy-start(f32[2304]{0:T(1024)} %param.13) | copy-start | bytes 27652
  59.2 0.6 copy-start.1
  412.6 12.6 copy-start.6
  412.6 12.6 copy-start.7
  446.4 19.1 %copy-start.9 = (pred[128,128]{0,1:T(8,128)(4,1)S(1)}, pred[128,128]{0,1:T(8,128)(4,1)}, u32[]{:S(2)}) copy-start(pred[128,128]{0,1:T(8,128)(4,1)} %iota_compare_fusion.2) | copy-start | bytes 49156
  557.8 35.4 %copy-start.11 = (f32[2304]{0:T(1024)S(1)}, f32[2304]{0:T(1024)}, u32[]{:S(2)}) copy-start(f32[2304]{0:T(1024)} %param.16) | copy-start | bytes 27652
  593.2 9.5 copy-start.3
  651.2 454.8 %all-to-all-start = ((bf16[8,640,2304]{2,1,0:T(8,128)(2,1)}), bf16[8,640,2304]{2,1,0:T(8,128)(2,1)}, u32[]{:S(2)}, u32[]{:S(2)}) async-start(bf16[8,640,2304]{2,1,0:T(8,128)(2,1)} %bitcast.55), calls=%async_computation | async-start | bytes 47185920 | tf_op jit(solution)/shard_map/all_to_all | solution.py:172
  656.3 759.7 %all-gather.14.cloned.1.call-start = ((), (), s32[]{:S(2)}) async-start(), calls=%async_computation.6 | async-start | bytes 39813120 | tf_op jit(solution)/shard_map/all_gather | solution.py:158
  1570.2 5.4 copy-start.2
  1570.2 6.4 copy-start.5
  1570.2 8.9 copy-start.8
  1570.2 261.5 %all-to-all-start.1 = ((bf16[8,640,2304]{2,1,0:T(8,128)(2,1)}), bf16[8,640,2304]{2,1,0:T(8,128)(2,1)}, u32[]{:S(2)}, u32[]{:S(2)}) async-start(bf16[8,640,2304]{2,1,0:T(8,128)(2,1)} %bitcast.56), calls=%async_computation.1 | async-start | bytes 47185920 | tf_op jit(solution)/shard_map/all_to_all | solution.py:175
Sparse Core Ops, SparseCore 0:
  22.8 150.8 all-gather.5
  175.5 57.9 all-gather.7
  235.0 308.4 all-gather.9
  544.9 561.0 all-gather.11
  1107.3 308.5 all-gather.13
